TPU v7x, 512 devices: a 4x2x32 block of a 4x8x32 slice. The times are simulated.
512 devices in a mesh: groups: 2 (over y), blk: 64 (over z, core), head: 4 (over x).
Axes of the slice: x: 4, y: 2, z: 32, core: 2. Of those that a mesh axis runs over, the one named last changes fastest.
The devices are a block of a 4x8x32 slice.
Arguments:
- queries: bfloat16 [4, 64, 8192], P('groups', 'blk', 'head'), parts along dimension 0, may hold values from -4.5 to 4.5
- stored_cache_keys: bfloat16 [4, 32768, 1024], P('groups', 'blk', 'head'), parts along dimension 0, may hold values from -4.5 to 4.5
- stored_cache_values: bfloat16 [4, 32768, 1024], P('groups', 'blk', 'head'), parts along dimension 0, may hold values from -6 to 6
- out_weight: bfloat16 [8192, 8192], P('head', 'blk'), may hold values from -3 to 3
- lengths: int32 [4], P('groups'), parts along dimension 0, may hold values from 16384 to 32768
Outputs:
- projected: bfloat16 [4, 64, 8192], P('groups', 'head', 'blk'), parts along dimension 0
There are 2 independent parts, one for each index of `groups`. A program takes and returns all parts, laid end to end along the dimension named above; an argument that names none is the same for every part. Nothing has to cross between parts.
All inputs are finite; a program needn't handle non-finite values.
Results may differ from a plain program's by a relative error of at most 0.0056.
Values may be sent and summed in bfloat16 or wider, within the bound.
No kernel may reach another device: no remote copies, remote signals or barrier semaphores. Data moves between devices by JAX's collectives and lax.ppermute only.
A program may use at most 64 MiB of HBM per device.

v0:
```python
import math

import jax
import jax.numpy as jnp
from jax import lax
from jax.sharding import Mesh
from jax.sharding import PartitionSpec as P

REQUEST_COUNT = 2
QUERY_HEAD_COUNT = 64
KEY_VALUE_HEADS = 8
HEAD_DIMENSION = 128
BLK = ("blk_0", "blk_1")


masked_fill_value = -1e30


def in_one_piece(arrays, axis, split_dim, concat_dim, along):
    ends, at = ([], 0)
    for a in arrays[:-1]:
        at += a.shape[along]
        ends.append(at)
    both = jnp.concatenate(arrays, axis=along)
    return tuple(
        jnp.split(
            lax.all_to_all(both, axis, split_axis=split_dim, concat_axis=concat_dim, tiled=True),
            ends,
            axis=along,
        )
    )


def joined_along(pieces, dim):
    shape = list(pieces.shape[1:])
    shape[dim] *= pieces.shape[0]
    return jnp.moveaxis(pieces, 0, dim).reshape(shape)


def gather_in_order(value, axes, order):
    pieces = value
    for k in order:
        pieces = lax.all_gather(pieces, axes[k])
    done = order[::-1]
    back = [done.index(k) for k in range(len(axes))]
    pieces = pieces.transpose(*back, *range(len(axes), pieces.ndim))
    return pieces.reshape(-1, *value.shape)


def gathered_by_axis(value, axes, order, dim):
    return joined_along(gather_in_order(value, axes, order), dim)


def in_blocks(value, dim, peers):
    before, after = (value.shape[:dim], value.shape[dim + 1 :])
    return jnp.moveaxis(value.reshape(*before, peers, -1, *after), dim, 0)


def sent_and_summed(value, axis, dim):
    pieces = in_blocks(value, dim, lax.axis_size(axis))
    arrived = lax.all_to_all(pieces, axis, split_axis=0, concat_axis=0, tiled=True)
    return arrived.sum(axis=0)


def body(queries, stored_cache_keys, stored_cache_values, out_weight, lengths):
    group_width = QUERY_HEAD_COUNT // KEY_VALUE_HEADS
    local_heads = stored_cache_keys.shape[2] // HEAD_DIMENSION
    query_heads = local_heads * group_width
    span = stored_cache_keys.shape[1]
    new_count = queries.shape[1] * lax.axis_size(BLK)
    key_pos = lax.axis_index(BLK) * span + jnp.arange(span, dtype=jnp.int32)
    score_scale = 1.0 / math.sqrt(HEAD_DIMENSION)
    piece = lax.all_gather(queries, BLK, axis=1, tiled=True)
    rows_count = piece.shape[1]
    query_pos = lengths[:, None] - new_count + jnp.arange(rows_count, dtype=jnp.int32)[None, :]
    sums_list = []
    maxima_list = []
    totals_list = []
    for request in range(REQUEST_COUNT):
        visible = (key_pos[None, :] <= query_pos[request][:, None])[:, None, :]
        parts_sum, parts_max, parts_total = ([], [], [])
        for kv_head in range(local_heads):
            block_query = piece[
                request,
                :,
                kv_head
                * group_width
                * HEAD_DIMENSION : (kv_head + 1)
                * group_width
                * HEAD_DIMENSION,
            ].reshape(rows_count, group_width, HEAD_DIMENSION)
            local_keys = stored_cache_keys[
                request, :, kv_head * HEAD_DIMENSION : (kv_head + 1) * HEAD_DIMENSION
            ]
            local_values = stored_cache_values[
                request, :, kv_head * HEAD_DIMENSION : (kv_head + 1) * HEAD_DIMENSION
            ]
            scores = (
                jnp.einsum(
                    "ngd,cd->ngc", block_query, local_keys, preferred_element_type=jnp.float32
                )
                * score_scale
            )
            block_max = jnp.max(jnp.where(visible, scores, masked_fill_value), axis=-1)
            weights = jnp.where(visible, jnp.exp(scores - block_max[..., None]), 0.0)
            parts_total.append(jnp.sum(weights, axis=-1))
            parts_max.append(block_max)
            weighted = jnp.einsum(
                "ngc,cd->ngd",
                weights.astype(jnp.bfloat16),
                local_values,
                preferred_element_type=jnp.float32,
            )
            parts_sum.append(weighted.reshape(rows_count, group_width * HEAD_DIMENSION))
        sums_list.append(jnp.concatenate(parts_sum, axis=1))
        maxima_list.append(jnp.concatenate(parts_max, axis=1))
        totals_list.append(jnp.concatenate(parts_total, axis=1))
    new_sums = jnp.stack(sums_list, axis=0)
    new_maxima = jnp.stack(maxima_list, axis=0)
    new_totals = jnp.stack(totals_list, axis=0)
    received = in_one_piece((new_sums[None], new_maxima[None], new_totals[None]), BLK, 2, 0, 3)
    part_sums, part_max, part_totals = received
    blocks = part_sums.shape[0]
    own_rows = part_sums.shape[2]
    top = jnp.max(part_max, axis=0)
    factor = jnp.exp(part_max - top[None])
    overall = jnp.sum(factor * part_totals, axis=0)
    shaped = part_sums.reshape(blocks, REQUEST_COUNT, own_rows, query_heads, HEAD_DIMENSION)
    merged = jnp.sum(shaped * factor[..., None], axis=0) / overall[..., None]
    own_attention = merged.astype(jnp.bfloat16).reshape(
        REQUEST_COUNT, own_rows, query_heads * HEAD_DIMENSION
    )
    terms = jnp.einsum(
        "rnc,cd->rnd",
        gathered_by_axis(own_attention, BLK, (0, 1), 1),
        out_weight,
        preferred_element_type=jnp.float32,
    )
    return sent_and_summed(terms, "head", 1).astype(jnp.bfloat16)


def solution(mesh):
    torus = Mesh(
        mesh.devices.reshape(mesh.shape["groups"], 32, 2, mesh.shape["head"]),
        ("groups", "blk_0", "blk_1", "head"),
    )
    return jax.shard_map(
        body,
        mesh=torus,
        in_specs=(
            P("groups", BLK, "head"),
            P("groups", BLK, "head"),
            P("groups", BLK, "head"),
            P("head", BLK),
            P("groups"),
        ),
        out_specs=P("groups", "head", BLK),
        check_vma=False,
    )
```

profile of v0, /device:TPU:33, one launch (start us, length us, event | category | flops | bytes accessed | tf_op | source)
XLA Modules:
  0.0 312.3 jit_solution(946098355099298313)
XLA Ops:
  0.0 0.7 broadcast_add_fusion
  0.8 98.4 %all_gather.12 = bf16[2,64,2048]{2,0,1:T(2,128)(2,1)S(1)} all-gather(bf16[2,1,2048]{2,0,1:T(2,128)(2,1)} %param.5), channel_id=1, replica_groups=mesh['groups'=2,'blk_0'=32,'blk_1'=2,'head'=4] {'blk_0','blk_1'}, dimensions={1}, use_global_device_ids=true | all-gather | bytes 532480 | tf_op jit(solution)/shard_map/all_gather | solution.py:73
  99.2 2.3 slice_reduce_fusion.3
  101.5 0.7 copy.35
  102.2 0.1 broadcast_compare_fusion.1
  102.3 1.3 select_reduce_fusion.1
  103.7 1.3 fusion.11
  105.0 2.1 fusion.5
  107.2 1.3 fusion.9
  108.5 1.3 select_reduce_fusion.3
  109.9 1.4 fusion.15
  111.4 2.6 fusion.1
  114.1 1.3 fusion.3
  115.4 1.3 fusion.13
  116.9 0.4 stack.28
  117.3 0.3 copy-done.6
  117.8 0.1 copy_bitcast_fusion.2
  118.0 0.4 stack.27
  118.6 0.9 maximum_bitcast_fusion
  119.5 2.1 concatenate.27
  121.7 121.2 %all_to_all.23 = f32[1,2,64,2080]{3,1,0,2:T(2,128)S(1)} all-to-all(f32[1,2,64,2080]{3,1,0,2:T(2,128)S(1)} %concatenate.27), channel_id=1, replica_groups=mesh['groups'=2,'blk_0'=32,'blk_1'=2,'head'=4] {'blk_0','blk_1'}, dimensions={2} | all-to-all | bytes 2129920 | tf_op jit(solution)/shard_map/all_to_all | solution.py:27
  243.0 0.1 fusion.47
  243.2 1.3 mul.43
  244.5 1.8 mul.44
  246.3 0.6 fusion
  246.9 39.0 %all_gather.13 = bf16[32,2,1,2048]{3,1,2,0:T(2,128)(2,1)S(1)} all-gather(bf16[1,2,1,2048]{3,1,2,0:T(2,128)(2,1)S(1)} %fusion.48), channel_id=1, replica_groups=mesh['groups'=2,'blk_0'=32,'blk_1'=2,'head'=4] {'blk_0'}, dimensions={0}, use_global_device_ids=true | all-gather | bytes 270336 | tf_op jit(solution)/shard_map/all_gather | solution.py:43
  286.0 16.1 %all-gather = bf16[64,2,1,2048]{3,0,1,2:T(8,128)(2,1)S(1)} all-gather(bf16[32,2,1,2048]{3,0,1,2:T(8,128)(2,1)S(1)} %copy.28), channel_id=2, replica_groups=mesh['groups'=2,'blk_0'=32,'blk_1'=2,'head'=4] {'blk_1'}, dimensions={0}, use_global_device_ids=true | all-gather | bytes 786432 | tf_op jit(solution)/shard_map/all_gather | solution.py:43
  302.1 0.5 copy.29
  302.6 0.2 copy.30
  302.8 0.3 convolution_bitcast_fusion
  303.1 8.6 %all_to_all.24 = f32[4,2,16,128]{3,2,1,0:T(8,128)S(1)} all-to-all(f32[4,2,16,128]{3,2,1,0:T(8,128)S(1)} %copy.31), channel_id=1, replica_groups=mesh['groups'=2,'blk_0'=32,'blk_1'=2,'head'=4] {'head'}, dimensions={0} | all-to-all | bytes 131072 | tf_op jit(solution)/shard_map/all_to_all | solution.py:61
  311.7 0.6 reduce_sum.72
  (43 shorter events, 1.3 us)
Async XLA Ops:
  0.0 302.8 %copy-start = (bf16[2048,128]{1,0:T(8,128)(2,1)S(1)}, bf16[2048,128]{1,0:T(8,128)(2,1)}, u32[]{:S(2)}) copy-start(bf16[2048,128]{1,0:T(8,128)(2,1)} %param.8) | copy-start | bytes 1572868
  109.8 1.5 copy-start.1
  109.8 1.5 copy-start.2
  115.4 1.3 copy-start.5
  116.9 0.8 copy-start.6
  116.9 0.8 copy-start.4
  116.9 0.9 copy-start.3
where the time goes:
time: 313 us; the launch traced here: 312 us
  blocking collectives  283 us (90%)
  matrix products  13 us (4%)
  local copies, waits for them, and re-layouts  11 us (4%)
  other arithmetic  4.7 us (2%)
    all_to_all x1, blocking collectives, in_one_piece(): lax.all_to_all(both, axis, split_axis=split_dim, concat_axis=concat_dim,...  121 us
    all_gather x1, blocking collectives, body(): piece = lax.all_gather(queries, BLK, axis=1, tiled=True)  98.4 us
    all_gather x2, blocking collectives, gather_in_order(): pieces = lax.all_gather(pieces, axes[k])  55.1 us
    all_to_all x1, blocking collectives, sent_and_summed(): lax.all_to_all(pieces, axis, split_axis=0, concat_axis=0, tiled=True)  8.57 us
    dot_general x4, matrix products, body(): jnp.einsum('ngd,cd->ngc', block_query, local_keys, preferred_element_type...  7.44 us

commit v1 on v0

v1 whole, which is shorter than its diff:
```python
import functools
import math

import jax
import jax.numpy as jnp
from jax import lax
from jax.experimental import pallas as pl
from jax.experimental.pallas import tpu as pltpu
from jax.sharding import Mesh
from jax.sharding import PartitionSpec as P

KEY_VALUE_HEADS = 8
HEAD_DIMENSION = 128
CORES = 2
BLK = ("z", "core")

masked_fill_value = -1e30
bf16 = jnp.bfloat16
f32 = jnp.float32


def attention_kernel(place, lengths, queries, own_keys, own_values, other_keys, other_values, out):
    new_count, requests, group, dim = queries.shape
    homes, per_home = out.shape[0], new_count // out.shape[0]
    span = own_keys.shape[1]
    rows = new_count * group
    kept = per_home * requests
    scale = 1.0 / math.sqrt(dim)
    lane = lax.broadcasted_iota(jnp.int32, (homes, group, dim), 2)
    stats = jnp.zeros((homes, group, dim), f32)
    token = lax.broadcasted_iota(jnp.int32, (rows, span), 0) // group
    column = lax.broadcasted_iota(jnp.int32, (rows, span), 1)
    for r in range(requests):
        q = queries[:, r].astype(f32).reshape(rows, dim).astype(bf16)
        last = lengths[r] - new_count
        keys = (own_keys[r], other_keys[pl.ds(r * span, span), :])
        values = (own_values[r], other_values[pl.ds(r * span, span), :])
        scores, seen = [], []
        top = None
        for part in range(2):
            s = lax.dot_general(q, keys[part], (((1,), (1,)), ((), ())), preferred_element_type=f32) * scale
            visible = column - token <= last - place[1 + part]
            s = jnp.where(visible, s, masked_fill_value)
            m = jnp.max(s, axis=1, keepdims=True)
            top = m if top is None else jnp.maximum(top, m)
            scores.append(s)
            seen.append(visible)
        shift = top.astype(bf16).astype(f32)
        total, summed = None, None
        for part in range(2):
            w = jnp.where(seen[part], jnp.exp(scores[part] - shift), 0.0)
            t = jnp.sum(w, axis=1, keepdims=True)
            o = jnp.dot(w.astype(bf16), values[part], preferred_element_type=f32)
            total = t if total is None else total + t
            summed = o if summed is None else summed + o
        high = total.astype(bf16).astype(f32)
        low = total - high
        summed = summed.reshape(homes, per_home, group, dim)
        for t in range(per_home):
            k = t * requests + r
            out[:, k] = summed[:, t].astype(bf16)
            for j, v in enumerate((shift, high, low)):
                v = v.reshape(homes, per_home, group, 1)[:, t]
                stats = jnp.where(lane == j * kept + k, v, stats)
    out[:, kept] = stats.astype(bf16)


def merge_kernel(parts, out):
    blocks, kept, dim = parts.shape[0], parts.shape[1] - 1, parts.shape[3]
    stats = parts[:, kept].astype(f32)
    factor = jnp.exp(stats - jnp.max(stats, axis=0, keepdims=True))
    group = stats.shape[1]
    flat = stats.reshape(blocks * group, dim)
    total = pltpu.roll(flat, dim - kept, 1) + pltpu.roll(flat, dim - 2 * kept, 1)
    total = jnp.sum(factor * total.reshape(stats.shape), axis=0)
    for k in range(kept):
        summed = jnp.sum(parts[:, k].astype(f32) * factor[:, :, k : k + 1], axis=0)
        row = (summed / total[:, k : k + 1]).astype(bf16)
        out[:, k] = jnp.broadcast_to(row[None], (blocks, group, dim))


def body(queries, stored_cache_keys, stored_cache_values, out_weight, lengths):
    requests, span, _ = stored_cache_keys.shape
    z_count, x_count = lax.axis_size("z"), lax.axis_size("head")
    new_count = queries.shape[1] * z_count * CORES
    dim = HEAD_DIMENSION
    group = queries.shape[2] // (CORES * dim)
    inputs = out_weight.shape[0] // CORES
    columns = out_weight.shape[1]
    z, core = lax.axis_index("z"), lax.axis_index("core")
    per_home = new_count // z_count
    kept = per_home * requests

    def head_of(cache, which):
        return lax.dynamic_slice_in_dim(cache, which * dim, dim, 2).reshape(requests * span, dim)

    leaving = jnp.concatenate(
        [
            head_of(stored_cache_keys, 1 - core),
            head_of(stored_cache_values, 1 - core),
            lax.dynamic_slice_in_dim(out_weight, (1 - core) * inputs, inputs, 0),
        ],
        axis=0,
    )
    arrived = lax.ppermute(leaving, "core", [(0, 1), (1, 0)])

    pieces = queries.reshape(requests, CORES, group, dim).transpose(1, 0, 2, 3)
    pieces = jnp.broadcast_to(pieces[None], (z_count, *pieces.shape)).reshape(-1, *pieces.shape[1:])
    all_queries = lax.all_to_all(pieces, BLK, 0, 0, tiled=True)

    place = jnp.stack([core, (z * CORES + core) * span, (z * CORES + 1 - core) * span]).astype(jnp.int32)
    rest = requests * span
    whole = lambda *shape: pl.BlockSpec(shape, lambda i, p, n: (0,) * len(shape))
    cache = pl.BlockSpec((requests, span, dim), lambda i, p, n: (0, 0, p[0]))
    partial = pl.pallas_call(
        attention_kernel,
        grid_spec=pltpu.PrefetchScalarGridSpec(
            num_scalar_prefetch=2,
            grid=(1,),
            in_specs=[
                whole(*all_queries.shape),
                cache,
                cache,
                pl.BlockSpec((rest, dim), lambda i, p, n: (0, 0)),
                pl.BlockSpec((rest, dim), lambda i, p, n: (1, 0)),
            ],
            out_specs=whole(z_count, kept + 1, group, dim),
        ),
        out_shape=jax.ShapeDtypeStruct((z_count, kept + 1, group, dim), bf16),
        name="attention",
    )(place, lengths, all_queries, stored_cache_keys, stored_cache_values, arrived, arrived)

    parts = lax.all_to_all(partial, "z", 0, 0, tiled=True)
    own = pl.pallas_call(
        merge_kernel,
        out_shape=jax.ShapeDtypeStruct((z_count, kept, group, dim), bf16),
        name="merge",
    )(parts)
    attention = lax.all_to_all(own, "z", 0, 0, tiled=True)

    mine = lax.dynamic_slice_in_dim(out_weight, core * inputs, inputs, 0)
    theirs = arrived[2 * rest :]
    first = core == 0
    weight = jnp.concatenate([jnp.where(first, mine, theirs), jnp.where(first, theirs, mine)], axis=1)
    terms = jnp.dot(
        attention.reshape(z_count * kept, group * dim), weight, preferred_element_type=f32
    )
    terms = terms.reshape(x_count, -1, CORES, columns).transpose(0, 2, 1, 3)
    terms = terms.reshape(x_count * CORES, -1, columns)
    terms = lax.all_to_all(terms, ("head", "core"), 0, 0, tiled=True).sum(axis=0)
    terms = terms.reshape(-1, requests, columns).transpose(1, 0, 2)
    return terms.astype(bf16)


def solution(mesh):
    shape = mesh.devices.shape
    torus = Mesh(
        mesh.devices.reshape(shape[0], shape[1] // CORES, CORES, shape[2]),
        ("groups", "z", "core", "head"),
    )
    return jax.shard_map(
        body,
        mesh=torus,
        in_specs=(
            P("groups", BLK, "head"),
            P("groups", BLK, "head"),
            P("groups", BLK, "head"),
            P("head", BLK),
            P("groups"),
        ),
        out_specs=P("groups", "head", BLK),
        check_vma=False,
    )
```

time: 313 us -> 207 us (0.66)
  blocking collectives: 283 us -> 64.8 us
  waiting for transfers between devices: 0 us -> 72.4 us
  starting transfers between devices: 0 us -> 55.9 us
  matrix products: 13 us -> 0.31 us
  Pallas kernels: 0 us -> 7.26 us
  local copies, waits for them, and re-layouts: 11 us -> 4.25 us
    all_gather x3 -> x0, blocking collectives: 153 us -> none  [the longest x1 98.4 us: body(): piece = lax.all_gather(queries, BLK, axis=1, tiled=True)]
    all_to_all x0 -> x2, waiting for transfers between devices: none -> 71.1 us  [the longest x1 36.2 us: body(): attention = lax.all_to_all(own, 'z', 0, 0, tiled=True)]
    all_to_all x2, blocking collectives: 130 us -> 64.8 us  [the longest x1 50.1 us: body(): parts = lax.all_to_all(partial, 'z', 0, 0, tiled=True)]
    all_to_all x0 -> x2, starting transfers between devices: none -> 52.7 us  [the longest x1 47.4 us: body(): all_queries = lax.all_to_all(pieces, BLK, 0, 0, tiled=True)]
    dot_general x9 -> x1, matrix products: 13 us -> 0.31 us  [body(): jnp.dot(attention.reshape(z_count * kept, group * dim), weight, preferred...]
    pallas_call x0 -> x2, Pallas kernels: none -> 7.26 us  [the longest x1 5.33 us: body(): pl.pallas_call(attention_kernel, grid_spec=pltpu.PrefetchScalarGridSpec(n...]
    ppermute x0 -> x1, starting transfers between devices: none -> 3.26 us  [body(): arrived = lax.ppermute(leaving, 'core', [(0, 1), (1, 0)])]
  transfers between devices with their start and end apart: 0 -> 3, of which waited for: 0 -> 3; matrix products, arithmetic and copies ran while one was open for 0% -> 1% of each run, Pallas kernels for 0% -> 0%
where the time goes in v1:
time: 207 us
  waiting for transfers between devices  72.4 us (35%)
  blocking collectives  64.8 us (31%)
  starting transfers between devices  55.9 us (27%)
  Pallas kernels  7.26 us (4%)
  local copies, waits for them, and re-layouts  4.25 us (2%)
    all_to_all x1, blocking collectives, body(): parts = lax.all_to_all(partial, 'z', 0, 0, tiled=True)  50.1 us
    all_to_all x1, starting transfers between devices, body(): all_queries = lax.all_to_all(pieces, BLK, 0, 0, tiled=True)  47.4 us
    all_to_all x1, waiting for transfers between devices, body(): attention = lax.all_to_all(own, 'z', 0, 0, tiled=True)  36.2 us
    all_to_all x1, waiting for transfers between devices, body(): all_queries = lax.all_to_all(pieces, BLK, 0, 0, tiled=True)  34.8 us
    all_to_all x1, blocking collectives, body(): lax.all_to_all(terms, ('head', 'core'), 0, 0, tiled=True).sum(axis=0)  14.7 us
    pallas_call x1, Pallas kernels, body(): pl.pallas_call(attention_kernel, grid_spec=pltpu.PrefetchScalarGridSpec(n...  5.33 us
    all_to_all x1, starting transfers between devices, body(): attention = lax.all_to_all(own, 'z', 0, 0, tiled=True)  5.23 us
  transfers between devices with their start and end apart: 3, of which 3 were waited for; matrix products, arithmetic and copies ran while one was open for 1% of the time, Pallas kernels for 0%

profile of v1, /device:TPU:33, one launch (start us, length us, event | category | flops | bytes accessed | tf_op | source)
XLA Modules:
  0.0 206.8 jit_solution(5701719838773072891)
XLA Ops:
  0.0 0.0 copy-start.1
  0.0 0.0 copy-start.2
  0.0 0.8 copy.15
  0.8 0.7 broadcast_in_dim.2
  1.5 47.4 %all-to-all-start = ((bf16[64,2,8,128]{3,2,1,0:T(8,128)(2,1)}), bf16[64,2,8,128]{3,2,1,0:T(8,128)(2,1)S(1)}, u32[]{:S(2)}, u32[]{:S(2)}) async-start(bf16[64,2,8,128]{3,2,1,0:T(8,128)(2,1)} %bitcast.4), calls=%async_computation | async-start | bytes 524288 | tf_op jit(solution)/shard_map/all_to_all | solution.py:109
  49.0 1.0 constant_dynamic-slice_fusion
  49.9 0.0 copy-done.1
  50.0 0.0 copy-done.2
  50.0 0.1 constant_dynamic-slice_fusion.1
  50.1 0.1 pad_maximum_fusion
  50.1 3.3 %collective-permute-start = (bf16[3072,128]{1,0:T(8,128)(2,1)S(1)}, bf16[3072,128]{1,0:T(8,128)(2,1)S(1)}, u32[]{:S(2)}, u32[]{:S(2)}) collective-permute-start(bf16[3072,128]{1,0:T(8,128)(2,1)S(1)} %pad_maximum_fusion), channel_id=1, source_target_pairs={{0,4},{4,0},{1,5},{5,1},{2,6},{6,2},{3,7},{7,3},{8,12},{12,8},{9,1... | collective-permute-start | bytes 2359304 | tf_op jit(solution)/shard_map/ppermute | solution.py:105
  53.4 0.6 pad_add_fusion.place
  54.0 1.3 collective-permute-done.other_keys.other_values
  55.3 0.0 copy-start
  55.3 34.8 %all-to-all-done.queries = bf16[64,2,8,128]{3,2,1,0:T(8,128)(2,1)S(1)} async-done(((bf16[64,2,8,128]{3,2,1,0:T(8,128)(2,1)}), bf16[64,2,8,128]{3,2,1,0:T(8,128)(2,1)S(1)}, u32[]{:S(2)}, u32[]{:S(2)}) %all-to-all-start) | async-done | bytes 262176 | tf_op jit(solution)/shard_map/all_to_all | solution.py:109
  90.1 0.0 copy-done
  90.1 0.0 copy-start.3
  90.1 0.7 copy-done.3
  90.8 5.3 %attention.1 = bf16[32,5,8,128]{3,2,1,0:T(8,128)(2,1)} custom-call(s32[3]{0:T(128)} %pad_add_fusion.place, s32[2]{0:T(128)} %lengths.1, bf16[64,2,8,128]{3,2,1,0:T(8,128)(2,1)} %copy-done.3, bf16[2,512,256]{2,1,0:T(8,128)(2,1)} %own_keys.1, bf16[2,512,256]{2,1,0:T(8,128)(2,1)} %own_values.1, bf16[3072,128]{1,0:T(8,128)(2,1)} %copy-done, ...), custom_call_target="tpu_custom_call" | custom-call | tf_op jit(solution)/shard_map/attention/pallas_call | solution.py:115
  96.2 0.0 copy-start.4
  96.2 50.1 %all_to_all.20.parts = bf16[32,5,8,128]{3,2,1,0:T(8,128)(2,1)} all-to-all(bf16[32,5,8,128]{3,2,1,0:T(8,128)(2,1)} %attention.1), channel_id=1, replica_groups=mesh['groups'=2,'z'=32,'core'=2,'head'=4] {'z'}, dimensions={0} | all-to-all | bytes 655360 | tf_op jit(solution)/shard_map/all_to_all | solution.py:133
  146.3 1.9 merge.1
  148.2 5.2 %all-to-all-start.2 = ((bf16[32,4,8,128]{3,2,1,0:T(8,128)(2,1)}), bf16[32,4,8,128]{3,2,1,0:T(8,128)(2,1)S(1)}, u32[]{:S(2)}, u32[]{:S(2)}) async-start(bf16[32,4,8,128]{3,2,1,0:T(8,128)(2,1)} %merge.1), calls=%async_computation.2 | async-start | bytes 524288 | tf_op jit(solution)/shard_map/all_to_all | solution.py:139
  153.5 0.0 copy-done.4
  153.5 1.1 broadcast_select_fusion.1
  154.5 0.1 maximum_bitcast_fusion
  154.6 0.2 copy.12
  154.8 36.2 %all-to-all-done.2 = bf16[32,4,8,128]{3,2,1,0:T(8,128)(2,1)S(1)} async-done(((bf16[32,4,8,128]{3,2,1,0:T(8,128)(2,1)}), bf16[32,4,8,128]{3,2,1,0:T(8,128)(2,1)S(1)}, u32[]{:S(2)}, u32[]{:S(2)}) %all-to-all-start.2) | async-done | bytes 262176 | tf_op jit(solution)/shard_map/all_to_all | solution.py:139
  191.1 0.1 reshape.28
  191.2 0.3 fusion
  191.5 14.7 %all_to_all.21 = f32[8,32,128]{2,1,0:T(8,128)S(1)} all-to-all(f32[8,32,128]{2,1,0:T(8,128)S(1)} %bitcast.36), channel_id=1, replica_groups=mesh['groups'=2,'z'=32,'core'=2,'head'=4] {'head','core'}, dimensions={0} | all-to-all | bytes 262144 | tf_op jit(solution)/shard_map/all_to_all | solution.py:150
  206.2 0.6 copy.10
  (2 shorter events, 0.0 us)
Async XLA Ops:
  0.0 49.9 %copy-start.1 = (bf16[2,512,256]{2,1,0:T(8,128)(2,1)S(1)}, bf16[2,512,256]{2,1,0:T(8,128)(2,1)}, u32[]{:S(2)}) copy-start(bf16[2,512,256]{2,1,0:T(8,128)(2,1)} %own_values.1) | copy-start | bytes 1572868
  0.0 50.0 %copy-start.2 = (bf16[2,512,256]{2,1,0:T(8,128)(2,1)S(1)}, bf16[2,512,256]{2,1,0:T(8,128)(2,1)}, u32[]{:S(2)}) copy-start(bf16[2,512,256]{2,1,0:T(8,128)(2,1)} %own_keys.1) | copy-start | bytes 1572868
  1.5 88.6 %all-to-all-start = ((bf16[64,2,8,128]{3,2,1,0:T(8,128)(2,1)}), bf16[64,2,8,128]{3,2,1,0:T(8,128)(2,1)S(1)}, u32[]{:S(2)}, u32[]{:S(2)}) async-start(bf16[64,2,8,128]{3,2,1,0:T(8,128)(2,1)} %bitcast.4), calls=%async_computation | async-start | bytes 524288 | tf_op jit(solution)/shard_map/all_to_all | solution.py:109
  50.1 5.2 %collective-permute-start = (bf16[3072,128]{1,0:T(8,128)(2,1)S(1)}, bf16[3072,128]{1,0:T(8,128)(2,1)S(1)}, u32[]{:S(2)}, u32[]{:S(2)}) collective-permute-start(bf16[3072,128]{1,0:T(8,128)(2,1)S(1)} %pad_maximum_fusion), channel_id=1, source_target_pairs={{0,4},{4,0},{1,5},{5,1},{2,6},{6,2},{3,7},{7,3},{8,12},{12,8},{9,1... | collective-permute-start | bytes 2359304 | tf_op jit(solution)/shard_map/ppermute | solution.py:105
  55.3 34.8 %copy-start = (bf16[3072,128]{1,0:T(8,128)(2,1)}, bf16[3072,128]{1,0:T(8,128)(2,1)S(1)}, u32[]{:S(2)}) copy-start(bf16[3072,128]{1,0:T(8,128)(2,1)S(1)} %collective-permute-done.other_keys.other_values) | copy-start | bytes 2359300
  90.1 0.7 copy-start.3
  96.2 57.3 %copy-start.4 = (bf16[2048,128]{1,0:T(8,128)(2,1)S(1)}, bf16[2048,128]{1,0:T(8,128)(2,1)}, u32[]{:S(2)}) copy-start(bf16[2048,128]{1,0:T(8,128)(2,1)} %param.8) | copy-start | bytes 1572868
  148.2 42.8 %all-to-all-start.2 = ((bf16[32,4,8,128]{3,2,1,0:T(8,128)(2,1)}), bf16[32,4,8,128]{3,2,1,0:T(8,128)(2,1)S(1)}, u32[]{:S(2)}, u32[]{:S(2)}) async-start(bf16[32,4,8,128]{3,2,1,0:T(8,128)(2,1)} %merge.1), calls=%async_computation.2 | async-start | bytes 524288 | tf_op jit(solution)/shard_map/all_to_all | solution.py:139

commit v2 on v1

--- a/solution.py
+++ b/solution.py
@@ -79,6 +79,21 @@
         out[:, k] = jnp.broadcast_to(row[None], (blocks, group, dim))
 
 
+def project_kernel(place, attention, mine, theirs, out, wide):
+    pieces, per_piece, columns = out.shape
+    inputs, dim = mine.shape[0], attention.shape[1]
+    group = inputs // dim
+    rows = attention.shape[0] // group
+    wide[...] = attention[...].astype(f32)
+    left = jnp.concatenate(
+        [wide[pl.ds(h, rows, stride=group), :].astype(bf16) for h in range(group)], axis=1
+    )
+    for weight, core in ((mine, place[0]), (theirs, 1 - place[0])):
+        terms = jnp.dot(left, weight[...], preferred_element_type=f32)
+        for x in range(pieces // CORES):
+            out[x * CORES + core] = terms[x * per_piece : (x + 1) * per_piece]
+
+
 def body(queries, stored_cache_keys, stored_cache_values, out_weight, lengths):
     requests, span, _ = stored_cache_keys.shape
     z_count, x_count = lax.axis_size("z"), lax.axis_size("head")
@@ -106,9 +121,10 @@
 
     pieces = queries.reshape(requests, CORES, group, dim).transpose(1, 0, 2, 3)
     pieces = jnp.broadcast_to(pieces[None], (z_count, *pieces.shape)).reshape(-1, *pieces.shape[1:])
+    place = jnp.stack([core, (z * CORES + core) * span, (z * CORES + 1 - core) * span]).astype(jnp.int32)
+    pieces, place, _ = lax.optimization_barrier((pieces, place, arrived))
     all_queries = lax.all_to_all(pieces, BLK, 0, 0, tiled=True)
 
-    place = jnp.stack([core, (z * CORES + core) * span, (z * CORES + 1 - core) * span]).astype(jnp.int32)
     rest = requests * span
     whole = lambda *shape: pl.BlockSpec(shape, lambda i, p, n: (0,) * len(shape))
     cache = pl.BlockSpec((requests, span, dim), lambda i, p, n: (0, 0, p[0]))
@@ -138,15 +154,23 @@
     )(parts)
     attention = lax.all_to_all(own, "z", 0, 0, tiled=True)
 
-    mine = lax.dynamic_slice_in_dim(out_weight, core * inputs, inputs, 0)
-    theirs = arrived[2 * rest :]
-    first = core == 0
-    weight = jnp.concatenate([jnp.where(first, mine, theirs), jnp.where(first, theirs, mine)], axis=1)
-    terms = jnp.dot(
-        attention.reshape(z_count * kept, group * dim), weight, preferred_element_type=f32
-    )
-    terms = terms.reshape(x_count, -1, CORES, columns).transpose(0, 2, 1, 3)
-    terms = terms.reshape(x_count * CORES, -1, columns)
+    rows = z_count * kept
+    terms = pl.pallas_call(
+        project_kernel,
+        grid_spec=pltpu.PrefetchScalarGridSpec(
+            num_scalar_prefetch=1,
+            grid=(1,),
+            in_specs=[
+                pl.BlockSpec((rows * group, dim), lambda i, p: (0, 0)),
+                pl.BlockSpec((inputs, columns), lambda i, p: (p[0], 0)),
+                pl.BlockSpec((inputs, columns), lambda i, p: (2 * rest // inputs, 0)),
+            ],
+            out_specs=pl.BlockSpec((x_count * CORES, rows // x_count, columns), lambda i, p: (0, 0, 0)),
+            scratch_shapes=[pltpu.VMEM((rows * group, dim), f32)],
+        ),
+        out_shape=jax.ShapeDtypeStruct((x_count * CORES, rows // x_count, columns), f32),
+        name="project",
+    )(place, attention.reshape(rows * group, dim), out_weight, arrived)
     terms = lax.all_to_all(terms, ("head", "core"), 0, 0, tiled=True).sum(axis=0)
     terms = terms.reshape(-1, requests, columns).transpose(1, 0, 2)
     return terms.astype(bf16)

time: 207 us -> 214 us (1.034)
  blocking collectives: 64.8 us -> 155 us
  waiting for transfers between devices: 72.4 us -> 1.19 us
  starting transfers between devices: 55.9 us -> 43.4 us
  Pallas kernels: 7.26 us -> 10 us
    all_to_all x0 -> x2, blocking collectives: none -> 89.1 us  [the longest x1 47.4 us: body(): all_queries = lax.all_to_all(pieces, BLK, 0, 0, tiled=True)]
    all_to_all x2 -> x0, waiting for transfers between devices: 71.1 us -> none  [the longest x1 36.2 us: body(): attention = lax.all_to_all(own, 'z', 0, 0, tiled=True)]
    all_to_all x2 -> x0, starting transfers between devices: 52.7 us -> none  [the longest x1 47.4 us: body(): all_queries = lax.all_to_all(pieces, BLK, 0, 0, tiled=True)]
    ppermute x1, starting transfers between devices: 3.26 us -> 43.4 us  [body(): arrived = lax.ppermute(leaving, 'core', [(0, 1), (1, 0)])]
    pallas_call x0 -> x1, Pallas kernels: none -> 2.78 us  [body(): pl.pallas_call(project_kernel, grid_spec=pltpu.PrefetchScalarGridSpec(num...]
  transfers between devices with their start and end apart: 3 -> 1, of which waited for: 3 -> 1; matrix products, arithmetic and copies ran while one was open for 1% -> 0% of each run, Pallas kernels for 0% -> 0%
where the time goes in v2:
time: 214 us; the launch traced here: 213 us
  blocking collectives  155 us (72%)
  starting transfers between devices  43.4 us (20%)
  Pallas kernels  10 us (5%)
  local copies, waits for them, and re-layouts  2.7 us (1%)
    all_to_all x1, blocking collectives, body(): parts = lax.all_to_all(partial, 'z', 0, 0, tiled=True)  50 us
    all_to_all x1, blocking collectives, body(): all_queries = lax.all_to_all(pieces, BLK, 0, 0, tiled=True)  47.4 us
    ppermute x1, starting transfers between devices, body(): arrived = lax.ppermute(leaving, 'core', [(0, 1), (1, 0)])  43.4 us
    all_to_all x1, blocking collectives, body(): attention = lax.all_to_all(own, 'z', 0, 0, tiled=True)  41.7 us
    all_to_all x1, blocking collectives, body(): lax.all_to_all(terms, ('head', 'core'), 0, 0, tiled=True).sum(axis=0)  16.2 us
    pallas_call x1, Pallas kernels, body(): pl.pallas_call(attention_kernel, grid_spec=pltpu.PrefetchScalarGridSpec(n...  5.32 us
  transfers between devices with their start and end apart: 1, of which 1 were waited for; matrix products, arithmetic and copies ran while one was open for 0% of the time, Pallas kernels for 0%

profile of v2, /device:TPU:33, one launch (start us, length us, event | category | flops | bytes accessed | tf_op | source)
XLA Modules:
  0.0 213.4 jit_solution(16155555568598542386)
XLA Ops:
  0.0 1.0 constant_dynamic-slice_fusion
  1.0 1.1 constant_dynamic-slice_fusion.1
  2.0 0.0 copy-start.1
  2.1 0.1 pad_maximum_fusion
  2.1 43.4 %collective-permute-start = (bf16[3072,128]{1,0:T(8,128)(2,1)S(1)}, bf16[3072,128]{1,0:T(8,128)(2,1)S(1)}, u32[]{:S(2)}, u32[]{:S(2)}) collective-permute-start(bf16[3072,128]{1,0:T(8,128)(2,1)S(1)} %pad_maximum_fusion), channel_id=1, source_target_pairs={{0,4},{4,0},{1,5},{5,1},{2,6},{6,2},{3,7},{7,3},{8,12},{12,8},{9,1... | collective-permute-start | bytes 2359304 | tf_op jit(solution)/shard_map/ppermute | solution.py:120
  45.5 0.0 copy-done.1
  45.5 0.7 pad_add_fusion.place
  46.2 1.2 collective-permute-done.other_keys.other_values.theirs
  47.4 0.0 copy-start
  47.4 47.4 %all_to_all.20.queries = bf16[64,2,8,128]{3,2,1,0:T(8,128)(2,1)} all-to-all(bf16[64,2,8,128]{3,2,1,0:T(8,128)(2,1)S(1)} %bitcast.21), channel_id=1, replica_groups=mesh['groups'=2,'z'=32,'core'=2,'head'=4] {'z','core'}, dimensions={0} | all-to-all | bytes 524288 | tf_op jit(solution)/shard_map/all_to_all | solution.py:126
  94.9 0.0 copy-done
  94.9 5.3 %attention.1 = bf16[32,5,8,128]{3,2,1,0:T(8,128)(2,1)} custom-call(s32[3]{0:T(128)} %pad_add_fusion.place, s32[2]{0:T(128)} %lengths.1, bf16[64,2,8,128]{3,2,1,0:T(8,128)(2,1)} %all_to_all.20.queries, bf16[2,512,256]{2,1,0:T(8,128)(2,1)} %own_keys.1, bf16[2,512,256]{2,1,0:T(8,128)(2,1)} %own_values.1, bf16[3072,128]{1,0:T(8,128)(2,1)} %copy-done, ...), custom_call_target="tpu_custom_call" | custom-call | tf_op jit(solution)/shard_map/attention/pallas_call | solution.py:131
  100.2 50.0 %all_to_all.21.parts = bf16[32,5,8,128]{3,2,1,0:T(8,128)(2,1)} all-to-all(bf16[32,5,8,128]{3,2,1,0:T(8,128)(2,1)} %attention.1), channel_id=1, replica_groups=mesh['groups'=2,'z'=32,'core'=2,'head'=4] {'z'}, dimensions={0} | all-to-all | bytes 655360 | tf_op jit(solution)/shard_map/all_to_all | solution.py:149
  150.2 1.9 merge.1
  152.1 41.7 %all_to_all.22 = bf16[32,4,8,128]{3,2,1,0:T(8,128)(2,1)} all-to-all(bf16[32,4,8,128]{3,2,1,0:T(8,128)(2,1)} %merge.1), channel_id=1, replica_groups=mesh['groups'=2,'z'=32,'core'=2,'head'=4] {'z'}, dimensions={0} | all-to-all | bytes 524288 | tf_op jit(solution)/shard_map/all_to_all | solution.py:155
  193.8 2.8 %project.1 = f32[8,32,128]{2,1,0:T(8,128)} custom-call(s32[3]{0:T(128)} %pad_add_fusion.place, bf16[1024,128]{1,0:T(8,128)(2,1)} %bitcast.20, bf16[2048,128]{1,0:T(8,128)(2,1)} %mine.1, bf16[3072,128]{1,0:T(8,128)(2,1)} %copy-done), custom_call_target="tpu_custom_call" | custom-call | tf_op jit(solution)/shard_map/project/pallas_call | solution.py:158
  196.6 16.2 %all_to_all.23 = f32[8,32,128]{2,1,0:T(8,128)S(1)} all-to-all(f32[8,32,128]{2,1,0:T(8,128)} %project.1), channel_id=1, replica_groups=mesh['groups'=2,'z'=32,'core'=2,'head'=4] {'head','core'}, dimensions={0} | all-to-all | bytes 262144 | tf_op jit(solution)/shard_map/all_to_all | solution.py:174
  212.8 0.6 copy.8
  (4 shorter events, 0.1 us)
Async XLA Ops:
  2.0 43.5 %copy-start.1 = (bf16[2,1,2048]{2,0,1:T(2,128)(2,1)S(1)}, bf16[2,1,2048]{2,0,1:T(2,128)(2,1)}, u32[]{:S(2)}) copy-start(bf16[2,1,2048]{2,0,1:T(2,128)(2,1)} %param.5) | copy-start | bytes 24580
  2.1 45.3 %collective-permute-start = (bf16[3072,128]{1,0:T(8,128)(2,1)S(1)}, bf16[3072,128]{1,0:T(8,128)(2,1)S(1)}, u32[]{:S(2)}, u32[]{:S(2)}) collective-permute-start(bf16[3072,128]{1,0:T(8,128)(2,1)S(1)} %pad_maximum_fusion), channel_id=1, source_target_pairs={{0,4},{4,0},{1,5},{5,1},{2,6},{6,2},{3,7},{7,3},{8,12},{12,8},{9,1... | collective-permute-start | bytes 2359304 | tf_op jit(solution)/shard_map/ppermute | solution.py:120
  47.4 47.5 %copy-start = (bf16[3072,128]{1,0:T(8,128)(2,1)}, bf16[3072,128]{1,0:T(8,128)(2,1)S(1)}, u32[]{:S(2)}) copy-start(bf16[3072,128]{1,0:T(8,128)(2,1)S(1)} %collective-permute-done.other_keys.other_values.theirs) | copy-start | bytes 2359300

commit v3 on v2

--- a/solution.py
+++ b/solution.py
@@ -1,4 +1,3 @@
-import functools
 import math
 
 import jax
@@ -19,13 +18,29 @@
 f32 = jnp.float32
 
 
-def attention_kernel(place, lengths, queries, own_keys, own_values, other_keys, other_values, out):
+def in_vmem(kernel, name, shape, dtype, **more):
+    def call(*arrays):
+        scalar = [a.dtype == jnp.int32 for a in arrays]
+        return pl.pallas_call(
+            kernel,
+            in_specs=[pl.BlockSpec(memory_space=pltpu.SMEM if s else pltpu.VMEM) for s in scalar],
+            out_specs=pl.BlockSpec(memory_space=pltpu.VMEM),
+            out_shape=pltpu.VMEM(shape, dtype),
+            name=name,
+            **more,
+        )(*(a if s else pltpu.with_memory_space_constraint(a, pltpu.VMEM) for a, s in zip(arrays, scalar)))
+
+    return call
+
+
+def attention_kernel(place, lengths, queries, own_keys, own_values, other, out):
     new_count, requests, group, dim = queries.shape
     homes, per_home = out.shape[0], new_count // out.shape[0]
     span = own_keys.shape[1]
     rows = new_count * group
     kept = per_home * requests
     scale = 1.0 / math.sqrt(dim)
+    head = pl.ds(pl.multiple_of(place[0] * dim, dim), dim)
     lane = lax.broadcasted_iota(jnp.int32, (homes, group, dim), 2)
     stats = jnp.zeros((homes, group, dim), f32)
     token = lax.broadcasted_iota(jnp.int32, (rows, span), 0) // group
@@ -33,8 +48,8 @@
     for r in range(requests):
         q = queries[:, r].astype(f32).reshape(rows, dim).astype(bf16)
         last = lengths[r] - new_count
-        keys = (own_keys[r], other_keys[pl.ds(r * span, span), :])
-        values = (own_values[r], other_values[pl.ds(r * span, span), :])
+        keys = (own_keys[r, :, head], other[pl.ds(r * span, span), :])
+        values = (own_values[r, :, head], other[pl.ds((requests + r) * span, span), :])
         scores, seen = [], []
         top = None
         for part in range(2):
@@ -79,17 +94,19 @@
         out[:, k] = jnp.broadcast_to(row[None], (blocks, group, dim))
 
 
-def project_kernel(place, attention, mine, theirs, out, wide):
+def project_kernel(place, attention, weight, other, out, wide):
     pieces, per_piece, columns = out.shape
-    inputs, dim = mine.shape[0], attention.shape[1]
+    inputs, dim = weight.shape[0] // CORES, attention.shape[1]
     group = inputs // dim
     rows = attention.shape[0] // group
     wide[...] = attention[...].astype(f32)
     left = jnp.concatenate(
         [wide[pl.ds(h, rows, stride=group), :].astype(bf16) for h in range(group)], axis=1
     )
-    for weight, core in ((mine, place[0]), (theirs, 1 - place[0])):
-        terms = jnp.dot(left, weight[...], preferred_element_type=f32)
+    mine = weight[pl.ds(pl.multiple_of(place[0] * inputs, inputs), inputs), :]
+    theirs = other[other.shape[0] - inputs :, :]
+    for right, core in ((mine, place[0]), (theirs, 1 - place[0])):
+        terms = jnp.dot(left, right, preferred_element_type=f32)
         for x in range(pieces // CORES):
             out[x * CORES + core] = terms[x * per_piece : (x + 1) * per_piece]
 
@@ -122,54 +139,23 @@
     pieces = queries.reshape(requests, CORES, group, dim).transpose(1, 0, 2, 3)
     pieces = jnp.broadcast_to(pieces[None], (z_count, *pieces.shape)).reshape(-1, *pieces.shape[1:])
     place = jnp.stack([core, (z * CORES + core) * span, (z * CORES + 1 - core) * span]).astype(jnp.int32)
-    pieces, place, _ = lax.optimization_barrier((pieces, place, arrived))
     all_queries = lax.all_to_all(pieces, BLK, 0, 0, tiled=True)
 
-    rest = requests * span
-    whole = lambda *shape: pl.BlockSpec(shape, lambda i, p, n: (0,) * len(shape))
-    cache = pl.BlockSpec((requests, span, dim), lambda i, p, n: (0, 0, p[0]))
-    partial = pl.pallas_call(
-        attention_kernel,
-        grid_spec=pltpu.PrefetchScalarGridSpec(
-            num_scalar_prefetch=2,
-            grid=(1,),
-            in_specs=[
-                whole(*all_queries.shape),
-                cache,
-                cache,
-                pl.BlockSpec((rest, dim), lambda i, p, n: (0, 0)),
-                pl.BlockSpec((rest, dim), lambda i, p, n: (1, 0)),
-            ],
-            out_specs=whole(z_count, kept + 1, group, dim),
-        ),
-        out_shape=jax.ShapeDtypeStruct((z_count, kept + 1, group, dim), bf16),
-        name="attention",
-    )(place, lengths, all_queries, stored_cache_keys, stored_cache_values, arrived, arrived)
+    partial = in_vmem(attention_kernel, "attention", (z_count, kept + 1, group, dim), bf16)(
+        place, lengths, all_queries, stored_cache_keys, stored_cache_values, arrived
+    )
 
     parts = lax.all_to_all(partial, "z", 0, 0, tiled=True)
-    own = pl.pallas_call(
-        merge_kernel,
-        out_shape=jax.ShapeDtypeStruct((z_count, kept, group, dim), bf16),
-        name="merge",
-    )(parts)
+    own = in_vmem(merge_kernel, "merge", (z_count, kept, group, dim), bf16)(parts)
     attention = lax.all_to_all(own, "z", 0, 0, tiled=True)
 
     rows = z_count * kept
-    terms = pl.pallas_call(
+    terms = in_vmem(
         project_kernel,
-        grid_spec=pltpu.PrefetchScalarGridSpec(
-            num_scalar_prefetch=1,
-            grid=(1,),
-            in_specs=[
-                pl.BlockSpec((rows * group, dim), lambda i, p: (0, 0)),
-                pl.BlockSpec((inputs, columns), lambda i, p: (p[0], 0)),
-                pl.BlockSpec((inputs, columns), lambda i, p: (2 * rest // inputs, 0)),
-            ],
-            out_specs=pl.BlockSpec((x_count * CORES, rows // x_count, columns), lambda i, p: (0, 0, 0)),
-            scratch_shapes=[pltpu.VMEM((rows * group, dim), f32)],
-        ),
-        out_shape=jax.ShapeDtypeStruct((x_count * CORES, rows // x_count, columns), f32),
-        name="project",
+        "project",
+        (x_count * CORES, rows // x_count, columns),
+        f32,
+        scratch_shapes=[pltpu.VMEM((rows * group, dim), f32)],
     )(place, attention.reshape(rows * group, dim), out_weight, arrived)
     terms = lax.all_to_all(terms, ("head", "core"), 0, 0, tiled=True).sum(axis=0)
     terms = terms.reshape(-1, requests, columns).transpose(1, 0, 2)

time: 214 us -> 203 us (0.949)
  blocking collectives: 155 us -> 107 us
  waiting for transfers between devices: 1.19 us -> 35.2 us
  starting transfers between devices: 43.4 us -> 50.7 us
  Pallas kernels: 10 us -> 4.62 us
    all_to_all x1 -> x0, blocking collectives: 47.4 us -> none  [body(): all_queries = lax.all_to_all(pieces, BLK, 0, 0, tiled=True)]
    all_to_all x0 -> x1, starting transfers between devices: none -> 47.4 us  [body(): all_queries = lax.all_to_all(pieces, BLK, 0, 0, tiled=True)]
    ppermute x1, starting transfers between devices: 43.4 us -> 3.25 us  [body(): arrived = lax.ppermute(leaving, 'core', [(0, 1), (1, 0)])]
    all_to_all x0 -> x1, waiting for transfers between devices: none -> 33.8 us  [body(): all_queries = lax.all_to_all(pieces, BLK, 0, 0, tiled=True)]
    pallas_call x3, Pallas kernels: 10 us -> 4.62 us  [call(): pl.pallas_call(kernel, in_specs=[pl.BlockSpec(memory_space=pltpu.SMEM if...]
  transfers between devices with their start and end apart: 1 -> 2, of which waited for: 1 -> 2; matrix products, arithmetic and copies ran while one was open for 0% -> 1% of each run, Pallas kernels for 0% -> 0%
where the time goes in v3:
time: 203 us; the launch traced here: 202 us
  blocking collectives  107 us (53%)
  starting transfers between devices  50.7 us (25%)
  waiting for transfers between devices  35.2 us (17%)
  Pallas kernels  4.62 us (2%)
  local copies, waits for them, and re-layouts  3.2 us (2%)
    all_to_all x1, blocking collectives, body(): parts = lax.all_to_all(partial, 'z', 0, 0, tiled=True)  49.2 us
    all_to_all x1, starting transfers between devices, body(): all_queries = lax.all_to_all(pieces, BLK, 0, 0, tiled=True)  47.4 us
    all_to_all x1, blocking collectives, body(): attention = lax.all_to_all(own, 'z', 0, 0, tiled=True)  42.7 us
    all_to_all x1, waiting for transfers between devices, body(): all_queries = lax.all_to_all(pieces, BLK, 0, 0, tiled=True)  33.8 us
    all_to_all x1, blocking collectives, body(): lax.all_to_all(terms, ('head', 'core'), 0, 0, tiled=True).sum(axis=0)  14.9 us
    pallas_call x3, Pallas kernels, call(): pl.pallas_call(kernel, in_specs=[pl.BlockSpec(memory_space=pltpu.SMEM if...  4.62 us
  transfers between devices with their start and end apart: 2, of which 2 were waited for; matrix products, arithmetic and copies ran while one was open for 1% of the time, Pallas kernels for 0%

profile of v3, /device:TPU:33, one launch (start us, length us, event | category | flops | bytes accessed | tf_op | source)
XLA Modules:
  0.0 202.3 jit_solution(11865708031821398324)
XLA Ops:
  0.0 0.0 copy-start
  0.0 0.0 copy-start.1
  0.0 0.8 copy.11
  0.8 0.7 broadcast_in_dim.2
  1.5 47.4 %all-to-all-start = ((bf16[64,2,8,128]{3,2,1,0:T(8,128)(2,1)}), bf16[64,2,8,128]{3,2,1,0:T(8,128)(2,1)S(1)}, u32[]{:S(2)}, u32[]{:S(2)}) async-start(bf16[64,2,8,128]{3,2,1,0:T(8,128)(2,1)} %bitcast.4), calls=%async_computation | async-start | bytes 524288 | tf_op jit(solution)/shard_map/all_to_all | solution.py:142
  49.0 0.0 copy-done
  49.0 0.0 copy-done.1
  49.0 1.0 constant_dynamic-slice_fusion.1
  50.1 0.0 copy-start.2
  50.1 0.0 copy-start.3
  50.1 0.9 pad_maximum_fusion
  51.0 3.3 %collective-permute-start = (bf16[3072,128]{1,0:T(8,128)(2,1)}, bf16[3072,128]{1,0:T(8,128)(2,1)S(1)}, u32[]{:S(2)}, u32[]{:S(2)}) collective-permute-start(bf16[3072,128]{1,0:T(8,128)(2,1)} %pad_maximum_fusion), channel_id=1, source_target_pairs={{0,4},{4,0},{1,5},{5,1},{2,6},{6,2},{3,7},{7,3},{8,12},{12,8},{9,1... | collective-permute-start | bytes 2359304 | tf_op jit(solution)/shard_map/ppermute | solution.py:137
  54.3 0.6 pad_add_fusion.place
  54.9 1.4 collective-permute-done.other
  56.4 33.8 %all-to-all-done.queries = bf16[64,2,8,128]{3,2,1,0:T(8,128)(2,1)S(1)} async-done(((bf16[64,2,8,128]{3,2,1,0:T(8,128)(2,1)}), bf16[64,2,8,128]{3,2,1,0:T(8,128)(2,1)S(1)}, u32[]{:S(2)}, u32[]{:S(2)}) %all-to-all-start) | async-done | bytes 262176 | tf_op jit(solution)/shard_map/all_to_all | solution.py:142
  90.1 0.0 copy-done.2
  90.1 0.0 copy-done.3
  90.1 3.3 %attention.1 = bf16[32,5,8,128]{3,2,1,0:T(8,128)(2,1)S(1)} custom-call(s32[3]{0:T(128)} %pad_add_fusion.place, s32[2]{0:T(128)} %lengths.1, bf16[64,2,8,128]{3,2,1,0:T(8,128)(2,1)S(1)} %all-to-all-done.queries, bf16[2,512,256]{2,1,0:T(8,128)(2,1)S(1)} %copy-done.2, bf16[2,512,256]{2,1,0:T(8,128)(2,1)S(1)} %copy-done.3, ...), custom_call_target="tpu_custom_call" | custom-call | tf_op jit(solution)/shard_map/attention/pallas_call | solution.py:24
  93.5 49.2 %all_to_all.20.parts = bf16[32,5,8,128]{3,2,1,0:T(8,128)(2,1)S(1)} all-to-all(bf16[32,5,8,128]{3,2,1,0:T(8,128)(2,1)S(1)} %attention.1), channel_id=1, replica_groups=mesh['groups'=2,'z'=32,'core'=2,'head'=4] {'z'}, dimensions={0} | all-to-all | bytes 655360 | tf_op jit(solution)/shard_map/all_to_all | solution.py:148
  142.7 0.3 merge.1
  143.0 42.7 %all_to_all.21 = bf16[32,4,8,128]{3,2,1,0:T(8,128)(2,1)S(1)} all-to-all(bf16[32,4,8,128]{3,2,1,0:T(8,128)(2,1)S(1)} %merge.1), channel_id=1, replica_groups=mesh['groups'=2,'z'=32,'core'=2,'head'=4] {'z'}, dimensions={0} | all-to-all | bytes 524288 | tf_op jit(solution)/shard_map/all_to_all | solution.py:150
  185.7 1.0 project.1
  186.7 14.9 %all_to_all.22 = f32[8,32,128]{2,1,0:T(8,128)S(1)} all-to-all(f32[8,32,128]{2,1,0:T(8,128)S(1)} %project.1), channel_id=1, replica_groups=mesh['groups'=2,'z'=32,'core'=2,'head'=4] {'head','core'}, dimensions={0} | all-to-all | bytes 262144 | tf_op jit(solution)/shard_map/all_to_all | solution.py:160
  201.7 0.6 copy.8
  (3 shorter events, 0.0 us)
Async XLA Ops:
  0.0 49.0 %copy-start = (bf16[2048,128]{1,0:T(8,128)(2,1)S(1)}, bf16[2048,128]{1,0:T(8,128)(2,1)}, u32[]{:S(2)}) copy-start(bf16[2048,128]{1,0:T(8,128)(2,1)} %weight.1) | copy-start | bytes 1572868
  0.0 49.0 %copy-start.1 = (bf16[2,512,256]{2,1,0:T(8,128)(2,1)S(1)}, bf16[2,512,256]{2,1,0:T(8,128)(2,1)}, u32[]{:S(2)}) copy-start(bf16[2,512,256]{2,1,0:T(8,128)(2,1)} %own_keys.1) | copy-start | bytes 1572868
  1.5 88.6 %all-to-all-start = ((bf16[64,2,8,128]{3,2,1,0:T(8,128)(2,1)}), bf16[64,2,8,128]{3,2,1,0:T(8,128)(2,1)S(1)}, u32[]{:S(2)}, u32[]{:S(2)}) async-start(bf16[64,2,8,128]{3,2,1,0:T(8,128)(2,1)} %bitcast.4), calls=%async_computation | async-start | bytes 524288 | tf_op jit(solution)/shard_map/all_to_all | solution.py:142
  50.1 40.1 %copy-start.2 = (bf16[2,512,256]{2,1,0:T(8,128)(2,1)S(1)}, bf16[2,512,256]{2,1,0:T(8,128)(2,1)}, u32[]{:S(2)}) copy-start(bf16[2,512,256]{2,1,0:T(8,128)(2,1)} %own_keys.1) | copy-start | bytes 1572868
  50.1 40.1 %copy-start.3 = (bf16[2,512,256]{2,1,0:T(8,128)(2,1)S(1)}, bf16[2,512,256]{2,1,0:T(8,128)(2,1)}, u32[]{:S(2)}) copy-start(bf16[2,512,256]{2,1,0:T(8,128)(2,1)} %own_values.1) | copy-start | bytes 1572868
  51.0 5.4 %collective-permute-start = (bf16[3072,128]{1,0:T(8,128)(2,1)}, bf16[3072,128]{1,0:T(8,128)(2,1)S(1)}, u32[]{:S(2)}, u32[]{:S(2)}) collective-permute-start(bf16[3072,128]{1,0:T(8,128)(2,1)} %pad_maximum_fusion), channel_id=1, source_target_pairs={{0,4},{4,0},{1,5},{5,1},{2,6},{6,2},{3,7},{7,3},{8,12},{12,8},{9,1... | collective-permute-start | bytes 2359304 | tf_op jit(solution)/shard_map/ppermute | solution.py:137

commit v4 on v3

--- a/solution.py
+++ b/solution.py
@@ -1,3 +1,4 @@
+import functools
 import math
 
 import jax
@@ -11,7 +12,8 @@
 KEY_VALUE_HEADS = 8
 HEAD_DIMENSION = 128
 CORES = 2
-BLK = ("z", "core")
+BLK = ("far", "near", "core")
+NEAR = 4
 
 masked_fill_value = -1e30
 bf16 = jnp.bfloat16
@@ -38,12 +40,15 @@
     homes, per_home = out.shape[0], new_count // out.shape[0]
     span = own_keys.shape[1]
     rows = new_count * group
+    far = homes // NEAR
     kept = per_home * requests
     scale = 1.0 / math.sqrt(dim)
     head = pl.ds(pl.multiple_of(place[0] * dim, dim), dim)
     lane = lax.broadcasted_iota(jnp.int32, (homes, group, dim), 2)
     stats = jnp.zeros((homes, group, dim), f32)
-    token = lax.broadcasted_iota(jnp.int32, (rows, span), 0) // group
+    home = lax.broadcasted_iota(jnp.int32, (rows, span), 0) // (group * per_home)
+    token = (home % far * NEAR + home // far) * per_home
+    token += lax.broadcasted_iota(jnp.int32, (rows, span), 0) // group % per_home
     column = lax.broadcasted_iota(jnp.int32, (rows, span), 1)
     for r in range(requests):
         q = queries[:, r].astype(f32).reshape(rows, dim).astype(bf16)
@@ -80,26 +85,49 @@
     out[:, kept] = stats.astype(bf16)
 
 
-def merge_kernel(parts, out):
-    blocks, kept, dim = parts.shape[0], parts.shape[1] - 1, parts.shape[3]
-    stats = parts[:, kept].astype(f32)
-    factor = jnp.exp(stats - jnp.max(stats, axis=0, keepdims=True))
-    group = stats.shape[1]
-    flat = stats.reshape(blocks * group, dim)
+def merged(parts):
+    kept, group, dim = parts.shape[-3] - 1, parts.shape[-2], parts.shape[-1]
+    stats = parts[..., kept, :, :].astype(f32)
+    shift = jnp.max(stats, axis=0)
+    factor = jnp.exp(stats - shift[None])
+    flat = stats.reshape(-1, dim)
     total = pltpu.roll(flat, dim - kept, 1) + pltpu.roll(flat, dim - 2 * kept, 1)
     total = jnp.sum(factor * total.reshape(stats.shape), axis=0)
+    rows = [
+        jnp.sum(parts[..., k, :, :].astype(f32) * factor[..., k : k + 1], axis=0) for k in range(kept)
+    ]
+    return rows, shift, total
+
+
+def merge_near_kernel(parts, out):
+    kept, group, dim = parts.shape[-3] - 1, parts.shape[-2], parts.shape[-1]
+    rows, shift, total = merged(parts)
     for k in range(kept):
-        summed = jnp.sum(parts[:, k].astype(f32) * factor[:, :, k : k + 1], axis=0)
-        row = (summed / total[:, k : k + 1]).astype(bf16)
-        out[:, k] = jnp.broadcast_to(row[None], (blocks, group, dim))
-
-
-def project_kernel(place, attention, weight, other, out, wide):
+        out[:, k] = rows[k].astype(bf16)
+    high = total.astype(bf16).astype(f32)
+    low = (total - high).reshape(-1, dim)
+    high = pltpu.roll(high.reshape(-1, dim), kept, 1).reshape(shift.shape)
+    low = pltpu.roll(low, 2 * kept, 1).reshape(shift.shape)
+    lane = lax.broadcasted_iota(jnp.int32, shift.shape, len(shift.shape) - 1)
+    out[:, kept] = jnp.where(lane < kept, shift, jnp.where(lane < 2 * kept, high, low)).astype(bf16)
+
+
+def merge_far_kernel(parts, out):
+    rows, _, total = merged(parts)
+    for k, row in enumerate(rows):
+        row = (row / total[:, k : k + 1]).astype(bf16)
+        out[:, k] = jnp.broadcast_to(row[None], (out.shape[0], *row.shape))
+
+
+def project_kernel(block, place, attention, weight, other, out, wide):
     pieces, per_piece, columns = out.shape
     inputs, dim = weight.shape[0] // CORES, attention.shape[1]
     group = inputs // dim
     rows = attention.shape[0] // group
-    wide[...] = attention[...].astype(f32)
+    homes = wide.shape[0] // block
+    for h in range(homes):
+        source = h % NEAR * (homes // NEAR) + h // NEAR
+        wide[h * block : (h + 1) * block] = attention[source * block : (source + 1) * block].astype(f32)
     left = jnp.concatenate(
         [wide[pl.ds(h, rows, stride=group), :].astype(bf16) for h in range(group)], axis=1
     )
@@ -111,15 +139,25 @@
             out[x * CORES + core] = terms[x * per_piece : (x + 1) * per_piece]
 
 
+def exchanged(pieces, axes):
+    flat = pieces.reshape(pieces.shape[0], -1, pieces.shape[-1])
+    return lax.all_to_all(flat, axes, 0, 0, tiled=True).reshape(pieces.shape)
+
+
+def shared(value, axis):
+    return exchanged(jnp.broadcast_to(value[None], (lax.axis_size(axis), *value.shape)), axis)
+
+
 def body(queries, stored_cache_keys, stored_cache_values, out_weight, lengths):
     requests, span, _ = stored_cache_keys.shape
-    z_count, x_count = lax.axis_size("z"), lax.axis_size("head")
+    far_count, x_count = lax.axis_size("far"), lax.axis_size("head")
+    z_count = far_count * NEAR
     new_count = queries.shape[1] * z_count * CORES
     dim = HEAD_DIMENSION
     group = queries.shape[2] // (CORES * dim)
     inputs = out_weight.shape[0] // CORES
     columns = out_weight.shape[1]
-    z, core = lax.axis_index("z"), lax.axis_index("core")
+    z, core = lax.axis_index(("far", "near")), lax.axis_index("core")
     per_home = new_count // z_count
     kept = per_home * requests
 
@@ -137,21 +175,25 @@
     arrived = lax.ppermute(leaving, "core", [(0, 1), (1, 0)])
 
     pieces = queries.reshape(requests, CORES, group, dim).transpose(1, 0, 2, 3)
-    pieces = jnp.broadcast_to(pieces[None], (z_count, *pieces.shape)).reshape(-1, *pieces.shape[1:])
+    pieces = jnp.broadcast_to(pieces[None], (far_count, *pieces.shape)).reshape(-1, *pieces.shape[1:])
+    all_queries = shared(exchanged(pieces, ("far", "core")), "near").reshape(new_count, requests, group, dim)
+
     place = jnp.stack([core, (z * CORES + core) * span, (z * CORES + 1 - core) * span]).astype(jnp.int32)
-    all_queries = lax.all_to_all(pieces, BLK, 0, 0, tiled=True)
 
     partial = in_vmem(attention_kernel, "attention", (z_count, kept + 1, group, dim), bf16)(
         place, lengths, all_queries, stored_cache_keys, stored_cache_values, arrived
     )
 
-    parts = lax.all_to_all(partial, "z", 0, 0, tiled=True)
-    own = in_vmem(merge_kernel, "merge", (z_count, kept, group, dim), bf16)(parts)
-    attention = lax.all_to_all(own, "z", 0, 0, tiled=True)
+    sent = partial.reshape(NEAR, far_count, *partial.shape[1:])
+    partial = in_vmem(merge_near_kernel, "merge_near", sent.shape[1:], bf16)(exchanged(sent, "near"))
+    own = in_vmem(merge_far_kernel, "merge_far", (far_count, kept, group, dim), bf16)(
+        exchanged(partial, "far")
+    )
+    attention = shared(exchanged(own, "far"), "near")
 
     rows = z_count * kept
     terms = in_vmem(
-        project_kernel,
+        functools.partial(project_kernel, kept * group),
         "project",
         (x_count * CORES, rows // x_count, columns),
         f32,
@@ -165,8 +207,8 @@
 def solution(mesh):
     shape = mesh.devices.shape
     torus = Mesh(
-        mesh.devices.reshape(shape[0], shape[1] // CORES, CORES, shape[2]),
-        ("groups", "z", "core", "head"),
+        mesh.devices.reshape(shape[0], -1, NEAR, CORES, shape[2]),
+        ("groups", "far", "near", "core", "head"),
     )
     return jax.shard_map(
         body,

time: 203 us -> 178 us (0.88)
  blocking collectives: 107 us -> 159 us
  starting transfers between devices: 50.7 us -> 5.43 us
  waiting for transfers between devices: 35.2 us -> 4.98 us
    all_to_all x2 -> x5, blocking collectives: 91.9 us -> 144 us  [exchanged(): return lax.all_to_all(flat, axes, 0, 0, tiled=True).reshape(pieces.shape)]
    all_to_all x1, starting transfers between devices: 47.4 us -> 3.5 us  [exchanged(): return lax.all_to_all(flat, axes, 0, 0, tiled=True).reshape(pieces.shape)]
    all_to_all x1, waiting for transfers between devices: 33.8 us -> 3.14 us  [exchanged(): return lax.all_to_all(flat, axes, 0, 0, tiled=True).reshape(pieces.shape)]
    pallas_call x3 -> x4, Pallas kernels: 4.62 us -> 4.75 us  [call(): pl.pallas_call(kernel, in_specs=[pl.BlockSpec(memory_space=pltpu.SMEM if...]
where the time goes in v4:
time: 178 us
  blocking collectives  159 us (89%)
  starting transfers between devices  5.43 us (3%)
  waiting for transfers between devices  4.98 us (3%)
  Pallas kernels  4.75 us (3%)
  local copies, waits for them, and re-layouts  2.3 us (1%)
    all_to_all x5, blocking collectives, exchanged(): return lax.all_to_all(flat, axes, 0, 0, tiled=True).reshape(pieces.shape)  144 us
    all_to_all x1, blocking collectives, body(): lax.all_to_all(terms, ('head', 'core'), 0, 0, tiled=True).sum(axis=0)  14.9 us
    pallas_call x4, Pallas kernels, call(): pl.pallas_call(kernel, in_specs=[pl.BlockSpec(memory_space=pltpu.SMEM if...  4.75 us
  transfers between devices with their start and end apart: 2, of which 2 were waited for; matrix products, arithmetic and copies ran while one was open for 1% of the time, Pallas kernels for 0%

profile of v4, /device:TPU:33, one launch (start us, length us, event | category | flops | bytes accessed | tf_op | source)
XLA Modules:
  0.0 177.9 jit_solution(6663454761746228136)
XLA Ops:
  0.0 0.0 copy-start
  0.0 0.8 copy.11
  0.8 0.0 copy-start.1
  0.8 0.0 copy-start.3
  0.8 71.0 %all_to_all.35 = bf16[16,16,128]{2,1,0:T(8,128)(2,1)S(1)} all-to-all(bf16[16,16,128]{2,1,0:T(8,128)(2,1)S(1)} %bitcast.39), channel_id=1, replica_groups=mesh['groups'=2,'far'=8,'near'=4,'core'=2,'head'=4] {'far','core'}, dimensions={0} | all-to-all | bytes 131072 | tf_op jit(solution)/shard_map/all_to_all | solution.py:144
  71.8 0.7 broadcast_in_dim.22
  72.6 3.5 %all-to-all-start.1 = ((bf16[4,256,128]{2,1,0:T(8,128)(2,1)}), bf16[4,256,128]{2,1,0:T(8,128)(2,1)S(1)}, u32[]{:S(2)}, u32[]{:S(2)}) async-start(bf16[4,256,128]{2,1,0:T(8,128)(2,1)} %broadcast_in_dim.22), calls=%async_computation.1 | async-start | bytes 524288 | tf_op jit(solution)/shard_map/all_to_all | solution.py:144
  76.1 0.0 copy-done
  76.1 0.0 copy-done.1
  76.1 0.0 copy-done.3
  76.1 0.1 constant_dynamic-slice_fusion.1
  76.3 0.0 copy-start.2
  76.3 0.0 copy-start.4
  76.3 0.9 pad_maximum_fusion
  77.2 1.9 %collective-permute-start = (bf16[3072,128]{1,0:T(8,128)(2,1)}, bf16[3072,128]{1,0:T(8,128)(2,1)S(1)}, u32[]{:S(2)}, u32[]{:S(2)}) collective-permute-start(bf16[3072,128]{1,0:T(8,128)(2,1)} %pad_maximum_fusion), channel_id=1, source_target_pairs={{0,4},{4,0},{1,5},{5,1},{2,6},{6,2},{3,7},{7,3},{8,12},{12,8},{9,1... | collective-permute-start | bytes 2359304 | tf_op jit(solution)/shard_map/ppermute | solution.py:175
  79.2 0.6 pad_add_fusion.place
  79.8 1.8 %collective-permute-done.other = bf16[3072,128]{1,0:T(8,128)(2,1)S(1)} collective-permute-done((bf16[3072,128]{1,0:T(8,128)(2,1)}, bf16[3072,128]{1,0:T(8,128)(2,1)S(1)}, u32[]{:S(2)}, u32[]{:S(2)}) %collective-permute-start) | collective-permute-done | bytes 786464 | tf_op jit(solution)/shard_map/ppermute | solution.py:175
  81.6 3.1 %all-to-all-done.1 = bf16[4,256,128]{2,1,0:T(8,128)(2,1)S(1)} async-done(((bf16[4,256,128]{2,1,0:T(8,128)(2,1)}), bf16[4,256,128]{2,1,0:T(8,128)(2,1)S(1)}, u32[]{:S(2)}, u32[]{:S(2)}) %all-to-all-start.1) | async-done | bytes 262176 | tf_op jit(solution)/shard_map/all_to_all | solution.py:144
  84.8 0.0 copy-done.2
  84.8 0.0 copy-done.4
  84.8 3.3 %attention.1 = bf16[32,5,8,128]{3,2,1,0:T(8,128)(2,1)S(1)} custom-call(s32[3]{0:T(128)} %pad_add_fusion.place, s32[2]{0:T(128)} %lengths.1, bf16[64,2,8,128]{3,2,1,0:T(8,128)(2,1)S(1)} %bitcast.30, bf16[2,512,256]{2,1,0:T(8,128)(2,1)S(1)} %copy-done.2, bf16[2,512,256]{2,1,0:T(8,128)(2,1)S(1)} %copy-done.4, bf16[3072,128]{1,0:T(8,128)(2,1)S(1)} %collective-permute-done.other), custom_call_target="tpu_custom_call" | custom-call | tf_op jit(solution)/shard_map/attention/pallas_call | solution.py:26
  88.1 11.4 %all_to_all.36 = bf16[4,320,128]{2,1,0:T(8,128)(2,1)S(1)} all-to-all(bf16[4,320,128]{2,1,0:T(8,128)(2,1)S(1)} %bitcast.28), channel_id=1, replica_groups=mesh['groups'=2,'far'=8,'near'=4,'core'=2,'head'=4] {'near'}, dimensions={0} | all-to-all | bytes 655360 | tf_op jit(solution)/shard_map/all_to_all | solution.py:144
  99.6 0.3 merge_near.1
  99.8 26.3 %all_to_all.37 = bf16[8,40,128]{2,1,0:T(8,128)(2,1)S(1)} all-to-all(bf16[8,40,128]{2,1,0:T(8,128)(2,1)S(1)} %bitcast.33), channel_id=1, replica_groups=mesh['groups'=2,'far'=8,'near'=4,'core'=2,'head'=4] {'far'}, dimensions={0} | all-to-all | bytes 163840 | tf_op jit(solution)/shard_map/all_to_all | solution.py:144
  126.1 0.2 merge_far.1
  126.2 25.9 %all_to_all.38 = bf16[8,32,128]{2,1,0:T(8,128)(2,1)S(1)} all-to-all(bf16[8,32,128]{2,1,0:T(8,128)(2,1)S(1)} %bitcast.34), channel_id=1, replica_groups=mesh['groups'=2,'far'=8,'near'=4,'core'=2,'head'=4] {'far'}, dimensions={0} | all-to-all | bytes 131072 | tf_op jit(solution)/shard_map/all_to_all | solution.py:144
  152.1 9.2 %all_to_all.39 = bf16[4,256,128]{2,1,0:T(8,128)(2,1)S(1)} all-to-all(bf16[4,256,128]{2,1,0:T(8,128)(2,1)S(1)} %broadcast_in_dim.24), channel_id=1, replica_groups=mesh['groups'=2,'far'=8,'near'=4,'core'=2,'head'=4] {'near'}, dimensions={0} | all-to-all | bytes 524288 | tf_op jit(solution)/shard_map/all_to_all | solution.py:144
  161.4 1.0 project.1
  162.4 14.9 %all_to_all.40 = f32[8,32,128]{2,1,0:T(8,128)S(1)} all-to-all(f32[8,32,128]{2,1,0:T(8,128)S(1)} %project.1), channel_id=1, replica_groups=mesh['groups'=2,'far'=8,'near'=4,'core'=2,'head'=4] {'head','core'}, dimensions={0} | all-to-all | bytes 262144 | tf_op jit(solution)/shard_map/all_to_all | solution.py:202
  177.3 0.6 copy.8
  (5 shorter events, 0.1 us)
Async XLA Ops:
  0.0 76.1 %copy-start = (bf16[2048,128]{1,0:T(8,128)(2,1)S(1)}, bf16[2048,128]{1,0:T(8,128)(2,1)}, u32[]{:S(2)}) copy-start(bf16[2048,128]{1,0:T(8,128)(2,1)} %weight.1) | copy-start | bytes 1572868
  0.8 75.3 %copy-start.1 = (bf16[2,512,256]{2,1,0:T(8,128)(2,1)S(1)}, bf16[2,512,256]{2,1,0:T(8,128)(2,1)}, u32[]{:S(2)}) copy-start(bf16[2,512,256]{2,1,0:T(8,128)(2,1)} %own_keys.1) | copy-start | bytes 1572868
  0.8 75.3 %copy-start.3 = (bf16[2,512,256]{2,1,0:T(8,128)(2,1)S(1)}, bf16[2,512,256]{2,1,0:T(8,128)(2,1)}, u32[]{:S(2)}) copy-start(bf16[2,512,256]{2,1,0:T(8,128)(2,1)} %own_values.1) | copy-start | bytes 1572868
  72.6 12.2 %all-to-all-start.1 = ((bf16[4,256,128]{2,1,0:T(8,128)(2,1)}), bf16[4,256,128]{2,1,0:T(8,128)(2,1)S(1)}, u32[]{:S(2)}, u32[]{:S(2)}) async-start(bf16[4,256,128]{2,1,0:T(8,128)(2,1)} %broadcast_in_dim.22), calls=%async_computation.1 | async-start | bytes 524288 | tf_op jit(solution)/shard_map/all_to_all | solution.py:144
  76.3 8.5 %copy-start.2 = (bf16[2,512,256]{2,1,0:T(8,128)(2,1)S(1)}, bf16[2,512,256]{2,1,0:T(8,128)(2,1)}, u32[]{:S(2)}) copy-start(bf16[2,512,256]{2,1,0:T(8,128)(2,1)} %own_keys.1) | copy-start | bytes 1572868
  76.3 8.5 %copy-start.4 = (bf16[2,512,256]{2,1,0:T(8,128)(2,1)S(1)}, bf16[2,512,256]{2,1,0:T(8,128)(2,1)}, u32[]{:S(2)}) copy-start(bf16[2,512,256]{2,1,0:T(8,128)(2,1)} %own_values.1) | copy-start | bytes 1572868
  77.2 4.4 %collective-permute-start = (bf16[3072,128]{1,0:T(8,128)(2,1)}, bf16[3072,128]{1,0:T(8,128)(2,1)S(1)}, u32[]{:S(2)}, u32[]{:S(2)}) collective-permute-start(bf16[3072,128]{1,0:T(8,128)(2,1)} %pad_maximum_fusion), channel_id=1, source_target_pairs={{0,4},{4,0},{1,5},{5,1},{2,6},{6,2},{3,7},{7,3},{8,12},{12,8},{9,1... | collective-permute-start | bytes 2359304 | tf_op jit(solution)/shard_map/ppermute | solution.py:175

commit v5 on v4

--- a/solution.py
+++ b/solution.py
@@ -9,7 +9,7 @@
 from jax.sharding import Mesh
 from jax.sharding import PartitionSpec as P
 
-KEY_VALUE_HEADS = 8
+
 HEAD_DIMENSION = 128
 CORES = 2
 BLK = ("far", "near", "core")
@@ -20,7 +20,7 @@
 f32 = jnp.float32
 
 
-def in_vmem(kernel, name, shape, dtype, **more):
+def in_vmem(kernel, shape, dtype, **more):
     def call(*arrays):
         scalar = [a.dtype == jnp.int32 for a in arrays]
         return pl.pallas_call(
@@ -28,7 +28,6 @@
             in_specs=[pl.BlockSpec(memory_space=pltpu.SMEM if s else pltpu.VMEM) for s in scalar],
             out_specs=pl.BlockSpec(memory_space=pltpu.VMEM),
             out_shape=pltpu.VMEM(shape, dtype),
-            name=name,
             **more,
         )(*(a if s else pltpu.with_memory_space_constraint(a, pltpu.VMEM) for a, s in zip(arrays, scalar)))
 
@@ -86,7 +85,7 @@
 
 
 def merged(parts):
-    kept, group, dim = parts.shape[-3] - 1, parts.shape[-2], parts.shape[-1]
+    kept, dim = parts.shape[-3] - 1, parts.shape[-1]
     stats = parts[..., kept, :, :].astype(f32)
     shift = jnp.max(stats, axis=0)
     factor = jnp.exp(stats - shift[None])
@@ -100,7 +99,7 @@
 
 
 def merge_near_kernel(parts, out):
-    kept, group, dim = parts.shape[-3] - 1, parts.shape[-2], parts.shape[-1]
+    kept, dim = parts.shape[-3] - 1, parts.shape[-1]
     rows, shift, total = merged(parts)
     for k in range(kept):
         out[:, k] = rows[k].astype(bf16)
@@ -115,12 +114,11 @@
 def merge_far_kernel(parts, out):
     rows, _, total = merged(parts)
     for k, row in enumerate(rows):
-        row = (row / total[:, k : k + 1]).astype(bf16)
-        out[:, k] = jnp.broadcast_to(row[None], (out.shape[0], *row.shape))
+        out[k] = (row / total[:, k : k + 1]).astype(bf16)
 
 
 def project_kernel(block, place, attention, weight, other, out, wide):
-    pieces, per_piece, columns = out.shape
+    pieces, per_piece, _ = out.shape
     inputs, dim = weight.shape[0] // CORES, attention.shape[1]
     group = inputs // dim
     rows = attention.shape[0] // group
@@ -174,27 +172,27 @@
     )
     arrived = lax.ppermute(leaving, "core", [(0, 1), (1, 0)])
 
+    place = jnp.stack([core, (z * CORES + core) * span, (z * CORES + 1 - core) * span]).astype(jnp.int32)
     pieces = queries.reshape(requests, CORES, group, dim).transpose(1, 0, 2, 3)
     pieces = jnp.broadcast_to(pieces[None], (far_count, *pieces.shape)).reshape(-1, *pieces.shape[1:])
-    all_queries = shared(exchanged(pieces, ("far", "core")), "near").reshape(new_count, requests, group, dim)
-
-    place = jnp.stack([core, (z * CORES + core) * span, (z * CORES + 1 - core) * span]).astype(jnp.int32)
-
-    partial = in_vmem(attention_kernel, "attention", (z_count, kept + 1, group, dim), bf16)(
+    some_queries = exchanged(pieces, ("far", "core"))
+    some_queries, arrived, place = lax.optimization_barrier((some_queries, arrived, place))
+    all_queries = shared(some_queries, "near").reshape(new_count, requests, group, dim)
+
+
+    partial = in_vmem(attention_kernel, (z_count, kept + 1, group, dim), bf16)(
         place, lengths, all_queries, stored_cache_keys, stored_cache_values, arrived
     )
 
     sent = partial.reshape(NEAR, far_count, *partial.shape[1:])
-    partial = in_vmem(merge_near_kernel, "merge_near", sent.shape[1:], bf16)(exchanged(sent, "near"))
-    own = in_vmem(merge_far_kernel, "merge_far", (far_count, kept, group, dim), bf16)(
-        exchanged(partial, "far")
-    )
-    attention = shared(exchanged(own, "far"), "near")
+    partial = in_vmem(merge_near_kernel, sent.shape[1:], bf16)(exchanged(sent, "near"))
+    own = in_vmem(merge_far_kernel, (kept, group, dim), bf16)(exchanged(partial, "far"))
+    attention = lax.all_gather(own.reshape(-1, dim), "far", axis=0, tiled=True)
+    attention = lax.all_gather(attention, "near", axis=0, tiled=True)
 
     rows = z_count * kept
     terms = in_vmem(
         functools.partial(project_kernel, kept * group),
-        "project",
         (x_count * CORES, rows // x_count, columns),
         f32,
         scratch_shapes=[pltpu.VMEM((rows * group, dim), f32)],

time: 178 us -> 195 us (1.096)
  blocking collectives: 159 us -> 113 us
  starting transfers between devices: 5.43 us -> 47.1 us
  waiting for transfers between devices: 4.98 us -> 25.5 us
    all_to_all x5 -> x3, blocking collectives: 144 us -> 49.6 us  [exchanged(): return lax.all_to_all(flat, axes, 0, 0, tiled=True).reshape(pieces.shape)]
    ppermute x1, starting transfers between devices: 1.94 us -> 43.5 us  [body(): arrived = lax.ppermute(leaving, 'core', [(0, 1), (1, 0)])]
    all_gather x0 -> x2, blocking collectives: none -> 40.5 us  [the longest x1 29.3 us: body(): attention = lax.all_gather(own.reshape(-1, dim), 'far', axis=0, tiled=True)]
    all_to_all x1, waiting for transfers between devices: 3.14 us -> 25.5 us  [exchanged(): return lax.all_to_all(flat, axes, 0, 0, tiled=True).reshape(pieces.shape)]
    all_to_all x1, blocking collectives: 14.9 us -> 22.5 us  [body(): lax.all_to_all(terms, ('head', 'core'), 0, 0, tiled=True).sum(axis=0)]
  transfers between devices with their start and end apart: 2 -> 2, of which waited for: 2 -> 1; matrix products, arithmetic and copies ran while one was open for 1% -> 1% of each run, Pallas kernels for 0% -> 0%
where the time goes in v5:
time: 195 us; the launch traced here: 194 us
  blocking collectives  113 us (58%)
  starting transfers between devices  47.1 us (24%)
  waiting for transfers between devices  25.5 us (13%)
  Pallas kernels  4.74 us (2%)
  local copies, waits for them, and re-layouts  3.34 us (2%)
    all_to_all x3, blocking collectives, exchanged(): return lax.all_to_all(flat, axes, 0, 0, tiled=True).reshape(pieces.shape)  49.6 us
    ppermute x1, starting transfers between devices, body(): arrived = lax.ppermute(leaving, 'core', [(0, 1), (1, 0)])  43.5 us
    all_gather x1, blocking collectives, body(): attention = lax.all_gather(own.reshape(-1, dim), 'far', axis=0, tiled=True)  29.3 us
    all_to_all x1, waiting for transfers between devices, exchanged(): return lax.all_to_all(flat, axes, 0, 0, tiled=True).reshape(pieces.shape)  25.5 us
    all_to_all x1, blocking collectives, body(): lax.all_to_all(terms, ('head', 'core'), 0, 0, tiled=True).sum(axis=0)  22.5 us
    all_gather x1, blocking collectives, body(): attention = lax.all_gather(attention, 'near', axis=0, tiled=True)  11.2 us
    pallas_call x4, Pallas kernels, call(): pl.pallas_call(kernel, in_specs=[pl.BlockSpec(memory_space=pltpu.SMEM if...  4.74 us
  transfers between devices with their start and end apart: 2, of which 1 were waited for; matrix products, arithmetic and copies ran while one was open for 1% of the time, Pallas kernels for 0%

profile of v5, /device:TPU:33, one launch (start us, length us, event | category | flops | bytes accessed | tf_op | source)
XLA Modules:
  0.0 194.1 jit_solution(18398487516375480708)
XLA Ops:
  0.0 1.0 constant_dynamic-slice_fusion
  1.0 1.1 constant_dynamic-slice_fusion.1
  2.0 0.0 copy-start.3
  2.1 0.1 pad_maximum_fusion
  2.1 0.0 copy-start.1
  2.1 0.0 copy-start.2
  2.1 43.5 %collective-permute-start = (bf16[3072,128]{1,0:T(8,128)(2,1)S(1)}, bf16[3072,128]{1,0:T(8,128)(2,1)S(1)}, u32[]{:S(2)}, u32[]{:S(2)}) collective-permute-start(bf16[3072,128]{1,0:T(8,128)(2,1)S(1)} %pad_maximum_fusion), channel_id=1, source_target_pairs={{0,4},{4,0},{1,5},{5,1},{2,6},{6,2},{3,7},{7,3},{8,12},{12,8},{9,1... | collective-permute-start | bytes 2359304 | tf_op jit(solution)/shard_map/ppermute | solution.py:173
  45.7 0.0 copy-done.3
  45.7 0.6 broadcast_in_dim.6
  46.3 3.6 %all-to-all-start = ((bf16[16,16,128]{2,1,0:T(8,128)(2,1)}), bf16[16,16,128]{2,1,0:T(8,128)(2,1)S(1)}, u32[]{:S(2)}, u32[]{:S(2)}) async-start(bf16[16,16,128]{2,1,0:T(8,128)(2,1)} %bitcast.1), calls=%async_computation | async-start | bytes 131072 | tf_op jit(solution)/shard_map/all_to_all | solution.py:142
  50.0 0.6 pad_add_fusion.place
  50.6 25.5 %all-to-all-done = bf16[16,16,128]{2,1,0:T(8,128)(2,1)S(1)} async-done(((bf16[16,16,128]{2,1,0:T(8,128)(2,1)}), bf16[16,16,128]{2,1,0:T(8,128)(2,1)S(1)}, u32[]{:S(2)}, u32[]{:S(2)}) %all-to-all-start) | async-done | bytes 65568 | tf_op jit(solution)/shard_map/all_to_all | solution.py:142
  76.1 0.0 collective-permute-done.other
  76.2 12.0 %all_to_all.25 = bf16[4,256,128]{2,1,0:T(8,128)(2,1)S(1)} all-to-all(bf16[4,256,128]{2,1,0:T(8,128)(2,1)S(1)} %broadcast_in_dim.16), channel_id=1, replica_groups=mesh['groups'=2,'far'=8,'near'=4,'core'=2,'head'=4] {'near'}, dimensions={0} | all-to-all | bytes 524288 | tf_op jit(solution)/shard_map/all_to_all | solution.py:142
  88.2 0.0 copy-done.1
  88.2 0.0 copy-done.2
  88.2 3.3 %shard_map.55 = bf16[32,5,8,128]{3,2,1,0:T(8,128)(2,1)S(1)} custom-call(s32[3]{0:T(128)} %pad_add_fusion.place, s32[2]{0:T(128)} %lengths.1, bf16[64,2,8,128]{3,2,1,0:T(8,128)(2,1)S(1)} %bitcast.29, bf16[2,512,256]{2,1,0:T(8,128)(2,1)S(1)} %copy-done.1, bf16[2,512,256]{2,1,0:T(8,128)(2,1)S(1)} %copy-done.2, bf16[3072,128]{1,0:T(8,128)(2,1)S(1)} %collective-permute-done.other), custom_call_target="tpu_custom_call" | custom-call | tf_op jit(solution)/shard_map/pallas_call | solution.py:26
  91.5 0.0 copy-start
  91.5 12.2 %all_to_all.26 = bf16[4,320,128]{2,1,0:T(8,128)(2,1)S(1)} all-to-all(bf16[4,320,128]{2,1,0:T(8,128)(2,1)S(1)} %bitcast.27), channel_id=1, replica_groups=mesh['groups'=2,'far'=8,'near'=4,'core'=2,'head'=4] {'near'}, dimensions={0} | all-to-all | bytes 655360 | tf_op jit(solution)/shard_map/all_to_all | solution.py:142
  103.7 0.3 shard_map.56
  103.9 25.5 %all_to_all.27 = bf16[8,40,128]{2,1,0:T(8,128)(2,1)S(1)} all-to-all(bf16[8,40,128]{2,1,0:T(8,128)(2,1)S(1)} %bitcast.31), channel_id=1, replica_groups=mesh['groups'=2,'far'=8,'near'=4,'core'=2,'head'=4] {'far'}, dimensions={0} | all-to-all | bytes 163840 | tf_op jit(solution)/shard_map/all_to_all | solution.py:142
  129.4 0.2 shard_map.57
  129.6 29.3 %all_gather.6 = bf16[256,128]{1,0:T(8,128)(2,1)S(1)} all-gather(bf16[32,128]{1,0:T(8,128)(2,1)S(1)} %bitcast.32), channel_id=1, replica_groups=mesh['groups'=2,'far'=8,'near'=4,'core'=2,'head'=4] {'far'}, dimensions={0}, use_global_device_ids=true | all-gather | bytes 73728 | tf_op jit(solution)/shard_map/all_gather | solution.py:190
  158.8 11.2 %all_gather.7.attention = bf16[1024,128]{1,0:T(8,128)(2,1)S(1)} all-gather(bf16[256,128]{1,0:T(8,128)(2,1)S(1)} %all_gather.6), channel_id=1, replica_groups=mesh['groups'=2,'far'=8,'near'=4,'core'=2,'head'=4] {'near'}, dimensions={0}, use_global_device_ids=true | all-gather | bytes 327680 | tf_op jit(solution)/shard_map/all_gather | solution.py:191
  170.0 0.0 copy-done
  170.0 1.0 shard_map.58
  171.1 22.5 %all_to_all.28 = f32[8,32,128]{2,1,0:T(8,128)S(1)} all-to-all(f32[8,32,128]{2,1,0:T(8,128)S(1)} %shard_map.58), channel_id=1, replica_groups=mesh['groups'=2,'far'=8,'near'=4,'core'=2,'head'=4] {'head','core'}, dimensions={0} | all-to-all | bytes 262144 | tf_op jit(solution)/shard_map/all_to_all | solution.py:200
  193.5 0.6 copy.8
  (4 shorter events, 0.1 us)
Async XLA Ops:
  2.0 43.6 %copy-start.3 = (bf16[2,1,2048]{2,0,1:T(2,128)(2,1)S(1)}, bf16[2,1,2048]{2,0,1:T(2,128)(2,1)}, u32[]{:S(2)}) copy-start(bf16[2,1,2048]{2,0,1:T(2,128)(2,1)} %param.5) | copy-start | bytes 24580
  2.1 86.0 %copy-start.1 = (bf16[2,512,256]{2,1,0:T(8,128)(2,1)S(1)}, bf16[2,512,256]{2,1,0:T(8,128)(2,1)}, u32[]{:S(2)}) copy-start(bf16[2,512,256]{2,1,0:T(8,128)(2,1)} %own_keys.1) | copy-start | bytes 1572868
  2.1 86.0 %copy-start.2 = (bf16[2,512,256]{2,1,0:T(8,128)(2,1)S(1)}, bf16[2,512,256]{2,1,0:T(8,128)(2,1)}, u32[]{:S(2)}) copy-start(bf16[2,512,256]{2,1,0:T(8,128)(2,1)} %own_values.1) | copy-start | bytes 1572868
  2.1 74.0 %collective-permute-start = (bf16[3072,128]{1,0:T(8,128)(2,1)S(1)}, bf16[3072,128]{1,0:T(8,128)(2,1)S(1)}, u32[]{:S(2)}, u32[]{:S(2)}) collective-permute-start(bf16[3072,128]{1,0:T(8,128)(2,1)S(1)} %pad_maximum_fusion), channel_id=1, source_target_pairs={{0,4},{4,0},{1,5},{5,1},{2,6},{6,2},{3,7},{7,3},{8,12},{12,8},{9,1... | collective-permute-start | bytes 2359304 | tf_op jit(solution)/shard_map/ppermute | solution.py:173
  46.3 29.8 %all-to-all-start = ((bf16[16,16,128]{2,1,0:T(8,128)(2,1)}), bf16[16,16,128]{2,1,0:T(8,128)(2,1)S(1)}, u32[]{:S(2)}, u32[]{:S(2)}) async-start(bf16[16,16,128]{2,1,0:T(8,128)(2,1)} %bitcast.1), calls=%async_computation | async-start | bytes 131072 | tf_op jit(solution)/shard_map/all_to_all | solution.py:142
  91.5 78.6 %copy-start = (bf16[2048,128]{1,0:T(8,128)(2,1)S(1)}, bf16[2048,128]{1,0:T(8,128)(2,1)}, u32[]{:S(2)}) copy-start(bf16[2048,128]{1,0:T(8,128)(2,1)} %weight.1) | copy-start | bytes 1572868
